TPU v7x, 32 devices: a whole 2x2x4 slice. The times are simulated.
32 devices in a mesh: beam: 2 (over x), tm: 16 (over z, y, core).
Axes of the slice: x: 2, y: 2, z: 4, core: 2. Of those that a mesh axis runs over, the one named last changes fastest.
Arguments:
- voltage: bfloat16 [2, 2, 2097152], P(None, None, ('beam', 'tm')), parts along dimension 2, may hold values from -11 to 11
- delays: int32 [64, 2048], replicated, may hold values from 0 to 96, as said below
- chan_mask: int32 [4096], P('beam'), parts along dimension 0, may hold values 0 or 1
Outputs:
- zscore: float32 [64, 1024], P(None, ('beam', 'tm')), parts along dimension 1
- trial_stats: float32 [3, 128], P(None, 'beam'), parts along dimension 1
There are 2 independent parts, one for each index of `beam`. A program takes and returns all parts, laid end to end along the dimension named above; an argument that names none is the same for every part. Nothing has to cross between parts.
Inputs may be any that keep to these rules, and one draw needn't show every extreme that they name: For each trial the delays never rise from one channel to the next; the last channel's delays are 0, and the first channel's delay of some trial is 96.
All inputs are finite; a program needn't handle non-finite values.
Results may differ from a plain program's by a relative error of at most 0.002.
Values may be sent and summed in bfloat16 or wider, within the bound.
No kernel may reach another device: no remote copies, remote signals or barrier semaphores. Data moves between devices by JAX's collectives and lax.ppermute only.
A program may use at most 64 MiB of HBM per device.

v0:
```python
import math
import jax
import jax.numpy as jnp
from jax import lax
from jax.sharding import PartitionSpec as P

NCHAN = 2048
TAPS = 16
DSPAN = 3
highest = lax.Precision.HIGHEST
shift_group = 8


def passed_along(value, axis, steps):
    count = lax.axis_size(axis)
    first, last = (max(0, -steps), min(count, count - steps))
    return lax.ppermute(value, axis, [(source, source + steps) for source in range(first, last)])


def prototype(tap_count, chan_count):
    length = tap_count * chan_count
    position = jnp.arange(length, dtype=jnp.float32)
    centred = (position - (length - 1) / 2.0) / chan_count
    window = 0.54 - 0.46 * jnp.cos(2.0 * jnp.pi * position / (length - 1))
    shaped = jnp.sinc(centred) * window
    shaped = shaped * jnp.sqrt(chan_count / jnp.sum(shaped * shaped))
    return shaped.reshape(tap_count, chan_count)


def phase_table(row_count, col_count, period):
    product = (
        jnp.arange(row_count, dtype=jnp.int32)[:, None]
        * jnp.arange(col_count, dtype=jnp.int32)[None, :]
        % period
    )
    angles = product.astype(jnp.float32) * (-2.0 * jnp.pi / period)
    return (jnp.cos(angles), jnp.sin(angles))


def spectral_power(weighted, chan_count):
    frame_count = weighted.shape[2]
    low_count = chan_count // 128
    split_up = weighted.reshape(2, 2, frame_count, low_count, 128)
    real_part = split_up[:, 0]
    imag_part = split_up[:, 1]
    cos_first, sin_first = phase_table(low_count, low_count, low_count)
    section_real = jnp.einsum(
        "pfmn,mk->pfkn", real_part, cos_first, precision=highest
    ) - jnp.einsum("pfmn,mk->pfkn", imag_part, sin_first, precision=highest)
    section_imag = jnp.einsum(
        "pfmn,mk->pfkn", real_part, sin_first, precision=highest
    ) + jnp.einsum("pfmn,mk->pfkn", imag_part, cos_first, precision=highest)
    cos_twist, sin_twist = phase_table(low_count, 128, chan_count)
    twist_real = section_real * cos_twist - section_imag * sin_twist
    twist_imag = section_real * sin_twist + section_imag * cos_twist
    cos_second, sin_second = phase_table(128, 128, 128)
    scale_factor = 1.0 / math.sqrt(chan_count)
    cos_second = cos_second * scale_factor
    sin_second = sin_second * scale_factor
    final_real = jnp.einsum(
        "pfkn,nj->pfkj", twist_real, cos_second, precision=highest
    ) - jnp.einsum("pfkn,nj->pfkj", twist_imag, sin_second, precision=highest)
    final_imag = jnp.einsum(
        "pfkn,nj->pfkj", twist_real, sin_second, precision=highest
    ) + jnp.einsum("pfkn,nj->pfkj", twist_imag, cos_second, precision=highest)
    energy = jnp.sum(final_real * final_real + final_imag * final_imag, axis=0)
    return jnp.transpose(energy, (2, 1, 0)).reshape(chan_count, frame_count).astype(jnp.bfloat16)


def dedisperse(padded, delays, out_width, max_delay):
    chan_count = padded.shape[0]
    group_count = (max_delay + shift_group) // shift_group
    needed = out_width + group_count * shift_group
    padded = jnp.concatenate(
        [padded, jnp.zeros((chan_count, needed - padded.shape[1]), padded.dtype)], axis=1
    )
    within = jnp.arange(shift_group, dtype=jnp.int32)

    def add_group(group_index, running):
        base = (group_index * shift_group).astype(jnp.int32)
        window = lax.dynamic_slice_in_dim(padded, base, out_width + shift_group - 1, 1)
        stacked = jnp.stack(
            [window[:, offset : offset + out_width] for offset in range(shift_group)]
        )
        targets = base + within
        selector = (delays[:, None, :] == targets[None, :, None]).astype(jnp.bfloat16)
        return running + jnp.einsum(
            "dsk,skt->dt", selector, stacked, preferred_element_type=jnp.float32
        )

    zero_sums = jnp.zeros((delays.shape[0], out_width), jnp.float32)
    return lax.fori_loop(0, group_count, add_group, zero_sums)


def per_device(voltage, delays, chan_mask):
    frame_count = voltage.shape[2] // NCHAN
    framed = voltage.reshape(2, 2, frame_count, NCHAN)
    history = passed_along(framed[:, :, frame_count - (TAPS - 1) :], "tm", 1)
    extended = jnp.concatenate([history, framed], axis=2)
    coeffs = prototype(TAPS, NCHAN)
    weighted = jnp.zeros((2, 2, frame_count, NCHAN), jnp.float32)
    for tap_index in range(TAPS):
        weighted = weighted + coeffs[tap_index] * extended[
            :, :, tap_index : tap_index + frame_count
        ].astype(jnp.float32)
    detected = spectral_power(weighted, NCHAN)
    masked = detected * chan_mask.astype(jnp.bfloat16)[:, None]
    max_delay = DSPAN * frame_count
    gathered = masked
    held_shards = 1
    while held_shards < DSPAN + 1:
        fetched = passed_along(gathered, "tm", -held_shards)
        gathered = jnp.concatenate([gathered, fetched], axis=1)
        held_shards = held_shards * 2
    series = dedisperse(gathered, delays, frame_count, max_delay)
    local_frames = series.shape[1]
    total_frames = local_frames * lax.axis_size("tm")
    totals = lax.psum(jnp.sum(series, axis=1), "tm")
    peak_value = lax.pmax(jnp.max(series, axis=1), "tm")
    average = totals / total_frames
    centred = series - average[:, None]
    variance = lax.psum(jnp.sum(centred * centred, axis=1), "tm") / total_frames
    deviation = jnp.sqrt(variance + 1e-05)
    zscore = centred / deviation[:, None]
    live_count = jnp.maximum(jnp.sum(chan_mask).astype(jnp.float32), 1.0)
    trial_stats = jnp.stack(
        [average / live_count, deviation / live_count, (peak_value - average) / deviation]
    )
    return (zscore, trial_stats)


def solution(mesh):
    in_specs = (P(None, None, ("beam", "tm")), P(), P("beam"))
    out_specs = (P(None, ("beam", "tm")), P(None, "beam"))
    return jax.shard_map(
        per_device, mesh=mesh, in_specs=in_specs, out_specs=out_specs, check_vma=False
    )
```

profile of v0, /device:TPU:0, one launch (start us, length us, event | category | flops | bytes accessed | tf_op | source)
XLA Modules:
  0.0 158.4 jit_solution(6258443623836400769)
XLA Ops:
  0.6 1.4 reshape.106
  2.2 2.4 %collective-permute-start = (bf16[2,2,15,2048]{3,2,0,1:T(8,128)(2,1)S(1)}, bf16[2,2,15,2048]{3,2,0,1:T(8,128)(2,1)S(1)}, u32[]{:S(2)}, u32[]{:S(2)}) collective-permute-start(bf16[2,2,15,2048]{3,2,0,1:T(8,128)(2,1)S(1)} %slice.217), channel_id=1, source_target_pairs={{0,1},{1,2},{2,3},{3,4},{4,5},{5,6},{6,7},{7,8},{8,9},{9,10},{10,1... | collective-permute-start | bytes 737288 | tf_op jit(solution)/shard_map/ppermute | solution.py:17
  4.6 1.2 multiply_reduce_fusion
  7.9 2.6 %multiply_add_fusion = f32[2,2,32,2048]{3,2,0,1:T(8,128)S(1)} fusion(bf16[2,2,32,2048]{3,2,0,1:T(8,128)(2,1)S(1)} %copy.12, bf16[2,2,15,2048]{3,2,0,1:T(8,128)(2,1)S(1)} %collective-permute-done, f32[2048]{0:T(1024)S(1)} %get-tuple-element.133, f32[2048]{0:T(1024)S(1)} %get-tuple-element.134, f32[2048]{0:T(1024)S(1)} %get-tuple-element.135, ...), kind=kLoop, calls=%fused_computation.61 | loop fusion | flops 24117248 | bytes 1949696 | tf_op jit(solution)/shard_map/add | solution.py:103
  17.4 1.3 collective-permute-start.1
  18.7 4.6 %collective-permute-done.1 = bf16[2048,32]{1,0:T(8,128)(2,1)S(1)} collective-permute-done((bf16[2048,32]{1,0:T(8,128)(2,1)S(1)}, bf16[2048,32]{1,0:T(8,128)(2,1)S(1)}, u32[]{:S(2)}, u32[]{:S(2)}) %collective-permute-start.1) | collective-permute-done | bytes 131104 | tf_op jit(solution)/shard_map/ppermute | solution.py:17
  23.6 1.5 collective-permute-start.2
  25.8 18.1 %collective-permute-done.2 = bf16[2048,64]{1,0:T(8,128)(2,1)S(1)} collective-permute-done((bf16[2048,64]{1,0:T(8,128)(2,1)S(1)}, bf16[2048,64]{1,0:T(8,128)(2,1)S(1)}, u32[]{:S(2)}, u32[]{:S(2)}) %collective-permute-start.2) | collective-permute-done | bytes 262176 | tf_op jit(solution)/shard_map/ppermute | solution.py:17
  43.9 0.9 maximum_maximum_fusion
  45.8 17.2 %while.14 = (s32[]{:T(128)}, f32[64,32]{0,1:T(8,128)S(1)}, s32[64,2048]{1,0:T(8,128)S(1)}, bf16[2048,136]{0,1:T(8,128)(2,1)S(1)}, s32[]{:T(128)}, /*index=5*/s32...) while((s32[]{:T(128)}, f32[64,32]{0,1:T(8,128)S(1)}, ...), condition=%wide.region_3.4_spmd.clone, body=%wide.region_2.3_spmd.clone.sunk | while | flops 68161560 | bytes 3686781 | solution.py:92
  46.2 0.9 fusion.178
  47.6 0.9 fusion.178
  48.9 0.9 fusion.178
  50.2 0.9 fusion.178
  51.6 0.9 fusion.178
  52.9 0.9 fusion.178
  54.2 0.9 fusion.178
  56.9 0.9 fusion.178
  58.2 0.9 fusion.178
  60.9 0.9 fusion.178
  62.2 0.9 fusion.178
  63.1 35.0 %psum.14 = f32[64]{0:T(128)S(1)} all-reduce(f32[64]{0:T(128)S(1)} %get-tuple-element.123), channel_id=1, replica_groups=mesh['beam'=2,'tm'=16] {'tm'}, use_global_device_ids=true, to_apply=%region_5.6 | all-reduce | flops 64 | bytes 512 | tf_op jit(solution)/shard_map/psum | solution.py:118
  98.2 29.5 %psum.15 = f32[64]{0:T(128)S(1)} all-reduce(f32[64]{0:T(128)S(1)} %multiply_reduce_fusion.1), channel_id=1, replica_groups=mesh['beam'=2,'tm'=16] {'tm'}, use_global_device_ids=true, to_apply=%region_7.8 | all-reduce | flops 64 | bytes 512 | tf_op jit(solution)/shard_map/psum | solution.py:122
  127.7 29.5 %pmax.7 = f32[64]{0:T(128)S(1)} all-reduce(f32[64]{0:T(128)S(1)} %get-tuple-element.122), channel_id=1, replica_groups=mesh['beam'=2,'tm'=16] {'tm'}, use_global_device_ids=true, to_apply=%region_10.11 | all-reduce | flops 64 | bytes 512 | tf_op jit(solution)/shard_map/pmax | solution.py:119
  (152 shorter events, 16.6 us)
Async XLA Ops:
  2.0 5.2 %copy-start = (s32[2048]{0:T(1024)S(1)}, s32[2048]{0:T(1024)}, u32[]{:S(2)}) copy-start(s32[2048]{0:T(1024)} %param.7) | copy-start | bytes 24580
  2.2 5.8 %collective-permute-start = (bf16[2,2,15,2048]{3,2,0,1:T(8,128)(2,1)S(1)}, bf16[2,2,15,2048]{3,2,0,1:T(8,128)(2,1)S(1)}, u32[]{:S(2)}, u32[]{:S(2)}) collective-permute-start(bf16[2,2,15,2048]{3,2,0,1:T(8,128)(2,1)S(1)} %slice.217), channel_id=1, source_target_pairs={{0,1},{1,2},{2,3},{3,4},{4,5},{5,6},{6,7},{7,8},{8,9},{9,10},{10,1... | collective-permute-start | bytes 737288 | tf_op jit(solution)/shard_map/ppermute | solution.py:17
  17.4 5.9 %collective-permute-start.1 = (bf16[2048,32]{1,0:T(8,128)(2,1)S(1)}, bf16[2048,32]{1,0:T(8,128)(2,1)S(1)}, u32[]{:S(2)}, u32[]{:S(2)}) collective-permute-start(bf16[2048,32]{1,0:T(8,128)(2,1)S(1)} %bitcast_multiply_fusion), channel_id=1, source_target_pairs={{1,0},{2,1},{3,2},{4,3},{5,4},{6,5},{7,6},{8,7},{9,8},{10,9},{11,1... | collective-permute-start | bytes 393224 | tf_op jit(solution)/shard_map/ppermute | solution.py:17
  23.6 20.3 %collective-permute-start.2 = (bf16[2048,64]{1,0:T(8,128)(2,1)S(1)}, bf16[2048,64]{1,0:T(8,128)(2,1)S(1)}, u32[]{:S(2)}, u32[]{:S(2)}) collective-permute-start(bf16[2048,64]{1,0:T(8,128)(2,1)S(1)} %pad_maximum_fusion.1), channel_id=1, source_target_pairs={{2,0},{3,1},{4,2},{5,3},{6,4},{7,5},{8,6},{9,7},{10,8},{11,9},{12,... | collective-permute-start | bytes 786440 | tf_op jit(solution)/shard_map/ppermute | solution.py:17
  44.8 1.0 copy-start.1
where the time goes:
time: 159 us; the launch traced here: 158 us
  blocking collectives  94 us (59%)
  waiting for transfers between devices  22.7 us (14%)
  matrix products  17.3 us (11%)
  other arithmetic  8.09 us (5%)
  local copies, waits for them, and re-layouts  7.21 us (5%)
  starting transfers between devices  5.18 us (3%)
  between operations  2.24 us (1%)
  loops' own time  1.66 us (1%)
    psum x1, blocking collectives, per_device(): totals = lax.psum(jnp.sum(series, axis=1), 'tm')  35 us
    psum x1, blocking collectives, per_device(): variance = lax.psum(jnp.sum(centred * centred, axis=1), 'tm') / total_frames  29.5 us
    pmax x1, blocking collectives, per_device(): peak_value = lax.pmax(jnp.max(series, axis=1), 'tm')  29.5 us
    ppermute x3, waiting for transfers between devices, passed_along(): lax.ppermute(value, axis, [(source, source + steps) for source in range(f...  22.7 us
    dot_general x13, matrix products, add_group(): jnp.einsum('dsk,skt->dt', selector, stacked, preferred_element_type=jnp.f...  11.5 us
    ppermute x3, starting transfers between devices, passed_along(): lax.ppermute(value, axis, [(source, source + steps) for source in range(f...  5.18 us
    while x91, local copies, waits for them, and re-layouts  3.45 us
  transfers between devices with their start and end apart: 3, of which 2 were waited for; matrix products, arithmetic and copies ran while one was open for 2% of the time, Pallas kernels for 0%

commit v1 on v0

--- a/solution.py
+++ b/solution.py
@@ -119,7 +119,8 @@
     peak_value = lax.pmax(jnp.max(series, axis=1), "tm")
     average = totals / total_frames
     centred = series - average[:, None]
-    variance = lax.psum(jnp.sum(centred * centred, axis=1), "tm") / total_frames
+    settle_spot = lambda state: jnp.sum(lax.all_gather(state, axis_name="tm"), axis=0)
+    variance = settle_spot(jnp.sum(centred * centred, axis=1)) / total_frames
     deviation = jnp.sqrt(variance + 1e-05)
     zscore = centred / deviation[:, None]
     live_count = jnp.maximum(jnp.sum(chan_mask).astype(jnp.float32), 1.0)

time: 159 us -> 159 us (level)
    psum x1 -> x0, blocking collectives: 29.5 us -> none  [per_device(): variance = lax.psum(jnp.sum(centred * centred, axis=1), 'tm') / total_frames]
    unnamed x0 -> x1, blocking collectives: none -> 29.5 us
where the time goes in v1:
time: 159 us
  blocking collectives  94 us (59%)
  waiting for transfers between devices  21.4 us (13%)
  matrix products  17.3 us (11%)
  local copies, waits for them, and re-layouts  8.13 us (5%)
  other arithmetic  8.11 us (5%)
  starting transfers between devices  5.18 us (3%)
  between operations  2.93 us (2%)
  loops' own time  1.66 us (1%)
    psum x1, blocking collectives, per_device(): totals = lax.psum(jnp.sum(series, axis=1), 'tm')  35 us
    pmax x1, blocking collectives, per_device(): peak_value = lax.pmax(jnp.max(series, axis=1), 'tm')  29.5 us
    unnamed x1, blocking collectives  29.5 us
    ppermute x3, waiting for transfers between devices, passed_along(): lax.ppermute(value, axis, [(source, source + steps) for source in range(f...  21.4 us
    dot_general x13, matrix products, add_group(): jnp.einsum('dsk,skt->dt', selector, stacked, preferred_element_type=jnp.f...  11.5 us
    ppermute x3, starting transfers between devices, passed_along(): lax.ppermute(value, axis, [(source, source + steps) for source in range(f...  5.18 us
    while x91, local copies, waits for them, and re-layouts  3.45 us
  transfers between devices with their start and end apart: 3, of which 2 were waited for; matrix products, arithmetic and copies ran while one was open for 2% of the time, Pallas kernels for 0%

profile of v1, /device:TPU:0, one launch (start us, length us, event | category | flops | bytes accessed | tf_op | source)
XLA Modules:
  0.0 158.7 jit_solution(12063745642957004767)
XLA Ops:
  0.6 1.4 reshape.133
  2.2 2.4 %collective-permute-start = (bf16[2,2,15,2048]{3,2,0,1:T(8,128)(2,1)S(1)}, bf16[2,2,15,2048]{3,2,0,1:T(8,128)(2,1)S(1)}, u32[]{:S(2)}, u32[]{:S(2)}) collective-permute-start(bf16[2,2,15,2048]{3,2,0,1:T(8,128)(2,1)S(1)} %slice.217), channel_id=1, source_target_pairs={{0,1},{1,2},{2,3},{3,4},{4,5},{5,6},{6,7},{7,8},{8,9},{9,10},{10,1... | collective-permute-start | bytes 737288 | tf_op jit(solution)/shard_map/ppermute | solution.py:17
  4.6 1.2 multiply_reduce_fusion
  7.9 2.6 %multiply_add_fusion = f32[2,2,32,2048]{3,2,0,1:T(8,128)S(1)} fusion(bf16[2,2,32,2048]{3,2,0,1:T(8,128)(2,1)S(1)} %copy.17, bf16[2,2,15,2048]{3,2,0,1:T(8,128)(2,1)S(1)} %collective-permute-done, f32[2048]{0:T(1024)S(1)} %get-tuple-element.137, f32[2048]{0:T(1024)S(1)} %get-tuple-element.138, f32[2048]{0:T(1024)S(1)} %get-tuple-element.139, ...), kind=kLoop, calls=%fused_computation.61 | loop fusion | flops 24117248 | bytes 1949696 | tf_op jit(solution)/shard_map/add | solution.py:103
  17.4 1.3 collective-permute-start.1
  18.7 4.6 %collective-permute-done.1 = bf16[2048,32]{1,0:T(8,128)(2,1)S(1)} collective-permute-done((bf16[2048,32]{1,0:T(8,128)(2,1)S(1)}, bf16[2048,32]{1,0:T(8,128)(2,1)S(1)}, u32[]{:S(2)}, u32[]{:S(2)}) %collective-permute-start.1) | collective-permute-done | bytes 131104 | tf_op jit(solution)/shard_map/ppermute | solution.py:17
  23.6 1.5 collective-permute-start.2
  27.0 16.8 %collective-permute-done.2 = bf16[2048,64]{1,0:T(8,128)(2,1)S(1)} collective-permute-done((bf16[2048,64]{1,0:T(8,128)(2,1)S(1)}, bf16[2048,64]{1,0:T(8,128)(2,1)S(1)}, u32[]{:S(2)}, u32[]{:S(2)}) %collective-permute-start.2) | collective-permute-done | bytes 262176 | tf_op jit(solution)/shard_map/ppermute | solution.py:17
  43.9 0.9 maximum_maximum_fusion
  45.9 17.2 %while.14 = (s32[]{:T(128)}, f32[64,32]{0,1:T(8,128)S(1)}, s32[64,2048]{1,0:T(8,128)S(1)}, bf16[2048,136]{0,1:T(8,128)(2,1)S(1)}, s32[]{:T(128)}, /*index=5*/s32...) while((s32[]{:T(128)}, f32[64,32]{0,1:T(8,128)S(1)}, ...), condition=%wide.region_3.4_spmd.clone, body=%wide.region_2.3_spmd.clone.sunk | while | flops 68161560 | bytes 3686781 | solution.py:92
  46.3 0.9 fusion.178
  47.6 0.9 fusion.178
  50.2 0.9 fusion.178
  51.6 0.9 fusion.178
  52.9 0.9 fusion.178
  54.2 0.9 fusion.178
  55.6 0.9 fusion.178
  56.9 0.9 fusion.178
  58.2 0.9 fusion.178
  59.5 0.9 fusion.178
  62.2 0.9 fusion.178
  63.1 35.0 %psum.7 = f32[64]{0:T(128)S(1)} all-reduce(f32[64]{0:T(128)S(1)} %get-tuple-element.127), channel_id=1, replica_groups=mesh['beam'=2,'tm'=16] {'tm'}, use_global_device_ids=true, to_apply=%region_5.6 | all-reduce | flops 64 | bytes 512 | tf_op jit(solution)/shard_map/psum | solution.py:118
  98.4 29.5 %all-reduce = f32[1024]{0:T(1024)S(1)} all-reduce(f32[1024]{0:T(1024)S(1)} %dynamic-update-slice), channel_id=2, replica_groups=mesh['beam'=2,'tm'=16] {'tm'}, use_global_device_ids=true, to_apply=%add | all-reduce | flops 1024 | bytes 8192
  128.0 29.5 %pmax.7 = f32[64]{0:T(128)S(1)} all-reduce(f32[64]{0:T(128)S(1)} %get-tuple-element.126), channel_id=1, replica_groups=mesh['beam'=2,'tm'=16] {'tm'}, use_global_device_ids=true, to_apply=%region_10.11 | all-reduce | flops 64 | bytes 512 | tf_op jit(solution)/shard_map/pmax | solution.py:119
  (159 shorter events, 17.6 us)
Async XLA Ops:
  2.0 5.2 %copy-start = (s32[2048]{0:T(1024)S(1)}, s32[2048]{0:T(1024)}, u32[]{:S(2)}) copy-start(s32[2048]{0:T(1024)} %param.7) | copy-start | bytes 24580
  2.2 5.8 %collective-permute-start = (bf16[2,2,15,2048]{3,2,0,1:T(8,128)(2,1)S(1)}, bf16[2,2,15,2048]{3,2,0,1:T(8,128)(2,1)S(1)}, u32[]{:S(2)}, u32[]{:S(2)}) collective-permute-start(bf16[2,2,15,2048]{3,2,0,1:T(8,128)(2,1)S(1)} %slice.217), channel_id=1, source_target_pairs={{0,1},{1,2},{2,3},{3,4},{4,5},{5,6},{6,7},{7,8},{8,9},{9,10},{10,1... | collective-permute-start | bytes 737288 | tf_op jit(solution)/shard_map/ppermute | solution.py:17
  17.4 8.4 %copy-start.2 = (u32[32]{0:T(128)S(1)}, u32[32]{0:T(128)}, u32[]{:S(2)}) copy-start(u32[32]{0:T(128)} %constant.151) | copy-start | bytes 388
  17.4 5.9 %collective-permute-start.1 = (bf16[2048,32]{1,0:T(8,128)(2,1)S(1)}, bf16[2048,32]{1,0:T(8,128)(2,1)S(1)}, u32[]{:S(2)}, u32[]{:S(2)}) collective-permute-start(bf16[2048,32]{1,0:T(8,128)(2,1)S(1)} %bitcast_multiply_fusion), channel_id=1, source_target_pairs={{1,0},{2,1},{3,2},{4,3},{5,4},{6,5},{7,6},{8,7},{9,8},{10,9},{11,1... | collective-permute-start | bytes 393224 | tf_op jit(solution)/shard_map/ppermute | solution.py:17
  23.6 20.3 %collective-permute-start.2 = (bf16[2048,64]{1,0:T(8,128)(2,1)S(1)}, bf16[2048,64]{1,0:T(8,128)(2,1)S(1)}, u32[]{:S(2)}, u32[]{:S(2)}) collective-permute-start(bf16[2048,64]{1,0:T(8,128)(2,1)S(1)} %pad_maximum_fusion.1), channel_id=1, source_target_pairs={{2,0},{3,1},{4,2},{5,3},{6,4},{7,5},{8,6},{9,7},{10,8},{11,9},{12,... | collective-permute-start | bytes 786440 | tf_op jit(solution)/shard_map/ppermute | solution.py:17
  44.8 1.0 copy-start.1
